TPU v7x, 16 devices: a whole 2x2x2 slice. The times are simulated.
16 devices in a mesh: dp: 1, tp: 16 (over x, y, z, core).
Axes of the slice: x: 2, y: 2, z: 2, core: 2. Of those that a mesh axis runs over, the one named last changes fastest.
Arguments:
- x: bfloat16 [1536, 12288], P(('dp', 'tp'))
- w: bfloat16 [12288, 32768], P(None, 'tp')
- label: int32 [1536], P(('dp', 'tp'))
Outputs:
- output 1: float32 [1536], P(('dp', 'tp'))
- output 2: bfloat16 [1536, 12288], P(('dp', 'tp'))
- output 3: bfloat16 [12288, 32768], P('dp', 'tp')
All inputs are finite; a program needn't handle non-finite values.
Results may differ from a plain program's by a relative error of at most 0.012.
Values are sent between devices in bfloat16 or wider.
A program may use at most 2 GiB of HBM per device.

v0:
```python
import jax
import jax.numpy as jnp
from jax import lax
from jax.sharding import PartitionSpec as P


def solution(mesh):
    def step(x, w, label):
        me, own_rows, columns = lax.axis_index("tp"), x.shape[0], w.shape[1]
        rows = lax.all_gather(x, "tp", axis=0, tiled=True)
        wanted = lax.all_gather(label, "tp", axis=0, tiled=True)
        logits = jnp.dot(rows, w, preferred_element_type=jnp.float32)
        hit = (wanted - me * columns)[:, None] == jnp.arange(columns, dtype=jnp.int32)[None, :]
        high = jnp.max(logits, -1)
        own = jnp.stack([high, jnp.sum(jnp.exp(logits - high[:, None]), -1), jnp.sum(jnp.where(hit, logits, 0.0), -1)])
        high, sums, right = jnp.moveaxis(lax.all_gather(own, "tp"), 1, 0)
        top = jnp.max(high, 0)
        total = jnp.sum(sums * jnp.exp(high - top), 0)
        loss = jnp.log(total) + top - jnp.sum(right, 0)
        e = jnp.exp(logits - top[:, None])
        by_logits = (e / total[:, None] - hit.astype(jnp.float32)).astype(jnp.bfloat16)
        term = jnp.dot(by_logits, w.T, preferred_element_type=jnp.float32).astype(jnp.bfloat16)
        by_x = lax.psum_scatter(term, "tp", scatter_dimension=0, tiled=True)
        by_w = jnp.dot(rows.T, by_logits, preferred_element_type=jnp.float32).astype(jnp.bfloat16)
        return lax.dynamic_slice_in_dim(loss, me * own_rows, own_rows), by_x, by_w

    return jax.shard_map(
        step,
        mesh=mesh,
        in_specs=(P(("dp", "tp"), None), P(None, "tp"), P(("dp", "tp"))),
        out_specs=(P(("dp", "tp")), P(("dp", "tp"), None), P("dp", "tp")),
        check_vma=False,
    )
```

profile of v0, /device:TPU:0, one launch (start us, length us, event | category | flops | bytes accessed | tf_op | source)
XLA Modules:
  0.0 572.0 jit_solution(8867239095676437633)
XLA Ops:
  7.2 0.0 all-gather.4.cloned.1.call-start
  7.2 0.7 all-gather.4.cloned.1.call-update
  7.9 0.0 reduce-scatter.2.cloned.1.call-start
  8.0 0.9 dynamic-update-slice
  8.8 35.3 %all-reduce = s32[1536]{0:T(1024)S(1)} all-reduce(s32[1536]{0:T(1024)S(1)} %dynamic-update-slice), channel_id=1, replica_groups=mesh['dp'=1,'tp'=16] {'tp'}, use_global_device_ids=true, to_apply=%add | all-reduce | flops 1536 | bytes 12288
  44.1 0.6 broadcast_subtract_fusion
  44.7 114.2 %all-gather.4.cloned.1.call-done = bf16[1536,12288]{1,0:T(8,128)(2,1)} async-done(((bf16[96,12288]{1,0:T(8,128)(2,1)}), bf16[1536,12288]{1,0:T(8,128)(2,1)}) %all-gather.4.cloned.1.call-update) | async-done | bytes 37748752 | tf_op jit(solution)/shard_map/all_gather | solution.py:10
  158.9 0.0 copy-start.3
  158.9 89.0 %fusion.3 = (f32[1536]{0:T(1024)S(1)}, f32[1536,2048]{1,0:T(8,128)}) fusion(bf16[1536,12288]{1,0:T(8,128)(2,1)} %all-gather.4.cloned.1.call-done, bf16[12288,2048]{1,0:T(8,128)(2,1)} %param.4), kind=kOutput, calls=%fused_computation.18 | convolution fusion | flops 77312557056 | bytes 100669440 | tf_op jit(solution)/shard_map/dot_general | solution.py:12
  247.9 0.0 copy-start
  247.9 0.0 copy-done.3
  247.9 8.0 %exponential_reduce_fusion = (f32[1536]{0:T(1024)S(1)}, f32[1536]{0:T(1024)S(1)}) fusion(f32[1536,2048]{1,0:T(8,128)} %get-tuple-element.16, f32[1536]{0:T(1024)S(1)} %get-tuple-element.15, s32[1536]{0:T(1024)S(1)} %copy-done.3), kind=kLoop, calls=%fused_computation.5 | loop fusion | flops 15725568 | bytes 12607488 | tf_op jit(solution)/shard_map/reduce_sum | solution.py:15
  256.0 13.6 %all-gather.1 = f32[16,3,1536]{2,1,0:T(4,128)S(1)} all-gather(f32[1,3,1536]{2,1,0:T(4,128)S(1)} %maximum_bitcast_fusion), channel_id=2, replica_groups=mesh['dp'=1,'tp'=16] {'tp'}, dimensions={0}, use_global_device_ids=true | all-gather | bytes 313344 | tf_op jit(solution)/shard_map/all_gather | solution.py:16
  269.6 0.8 slice_reduce_fusion.1
  270.4 0.0 copy-start.1
  270.5 0.6 copy-done.1
  271.0 0.0 copy-start.5
  271.0 0.6 copy-done.5
  271.6 0.0 copy-done
  271.6 5.3 subtract_convert_fusion.7
  276.9 87.0 %convolution_convert_fusion = bf16[1536,12288]{1,0:T(8,128)(2,1)} fusion(bf16[12288,2048]{1,0:T(8,128)(2,1)} %param.4, bf16[1536,2048]{1,0:T(8,128)(2,1)} %subtract_convert_fusion.7), kind=kOutput, calls=%fused_computation.1 | convolution fusion | flops 77328285696 | bytes 94371840 | tf_op jit(solution)/shard_map/dot_general | solution.py:22
  363.9 0.0 copy-start.2
  363.9 0.0 copy-start.4
  364.0 0.0 copy-start.6
  364.0 0.0 reduce-scatter.2.cloned.1.call-update
  364.0 0.7 copy-done.2
  364.6 0.0 copy-done.4
  364.7 0.0 copy-done.6
  364.7 103.2 %convert_bitcast_fusion = bf16[12288,2048]{0,1:T(8,128)(2,1)} fusion(bf16[1536,12288]{1,0:T(8,128)(2,1)} %all-gather.4.cloned.1.call-done, f32[1536,2048]{1,0:T(8,128)} %get-tuple-element.16, f32[1536]{0:T(1024)S(1)} %copy-done.6, f32[1536]{0:T(1024)S(1)} %copy-done.2, s32[1536]{0:T(1024)S(1)} %copy-done.4), kind=kOutput, calls=%fused_computation | convolution fusion | flops 77353451520 | bytes 100681728 | tf_op jit(solution)/shard_map/dot_general | solution.py:24
  467.9 64.5 %copy.9 = bf16[12288,2048]{1,0:T(8,128)(2,1)} copy(bf16[12288,2048]{0,1:T(8,128)(2,1)} %convert_bitcast_fusion) | data formatting | bytes 100663296
  532.4 1.3 dynamic-slice_subtract_fusion
  533.7 31.5 %reduce-scatter.2.cloned.1.call-done = bf16[96,12288]{1,0:T(8,128)(2,1)} async-done(((bf16[1536,12288]{1,0:T(8,128)(2,1)}), bf16[96,12288]{1,0:T(8,128)(2,1)}) %reduce-scatter.2.cloned.1.call-update) | async-done | bytes 2359312 | tf_op jit(solution)/shard_map/reduce_scatter | solution.py:23
  (6 shorter events, 0.1 us)
Async XLA Ops:
  7.2 151.7 %all-gather.4.cloned.1.call-start = ((), (), s32[]{:S(2)}) async-start(), calls=%async_computation.1 | async-start | bytes 40108032 | tf_op jit(solution)/shard_map/all_gather | solution.py:10
  7.9 557.3 %reduce-scatter.2.cloned.1.call-start = ((), (), s32[]{:S(2)}) async-start(), calls=%async_computation.2 | async-start | bytes 40108032 | tf_op jit(solution)/shard_map/reduce_scatter | solution.py:23
  158.9 89.1 %copy-start.3 = (s32[1536]{0:T(1024)S(1)}, s32[1536]{0:T(1024)}, u32[]{:S(2)}) copy-start(s32[1536]{0:T(1024)} %broadcast_subtract_fusion) | copy-start | bytes 18436
  247.9 23.7 %copy-start = (f32[1536,2048]{1,0:T(8,128)S(1)}, f32[1536,2048]{1,0:T(8,128)}, u32[]{:S(2)}) copy-start(f32[1536,2048]{1,0:T(8,128)} %get-tuple-element.16) | copy-start | bytes 37748740
  270.4 0.6 copy-start.1
  271.0 0.6 copy-start.5
  363.9 0.7 copy-start.2
  363.9 0.7 copy-start.4
  364.0 0.7 copy-start.6
Sparse Core Ops, SparseCore 0:
  10.2 148.6 all-gather.3
  364.1 201.0 reduce-scatter.1
where the time goes:
time: 574 us; the launch traced here: 572 us
  matrix products  279 us (49%)
  waiting for transfers between devices  146 us (25%)
  local copies, waits for them, and re-layouts  67.3 us (12%)
  blocking collectives  48.8 us (9%)
  other arithmetic  16.1 us (3%)
  between operations  14.1 us (2%)
    all_gather x1, waiting for transfers between devices, step(): rows = lax.all_gather(x, 'tp', axis=0, tiled=True)  114 us
    dot_general x1, matrix products, step(): jnp.dot(rows.T, by_logits, preferred_element_type=jnp.float32)  103 us
    dot_general x1, matrix products, step(): logits = jnp.dot(rows, w, preferred_element_type=jnp.float32)  89 us
    dot_general x1, matrix products, step(): jnp.dot(by_logits, w.T, preferred_element_type=jnp.float32)  87 us
    unnamed x17, local copies, waits for them, and re-layouts  67.2 us
    unnamed x1, blocking collectives  35.3 us
    reduce_scatter x1, waiting for transfers between devices, step(): by_x = lax.psum_scatter(term, 'tp', scatter_dimension=0, tiled=True)  31.5 us
    all_gather x1, blocking collectives, step(): high, sums, right = jnp.moveaxis(lax.all_gather(own, 'tp'), 1, 0)  13.6 us
  transfers between devices with their start and end apart: 2, of which 2 were waited for; matrix products, arithmetic and copies ran while one was open for 30% of the time, Pallas kernels for 0%

commit v1 on v0

v1 whole, which is shorter than its diff:
```python
import functools

import jax
import jax.numpy as jnp
from jax import lax
from jax.experimental import pallas as pl
from jax.experimental.pallas import tpu as pltpu
from jax.sharding import PartitionSpec as P

MESH = pl.DeviceIdType.MESH
F32, BF16 = jnp.float32, jnp.bfloat16


def _where_am_i():
    me = lax.axis_index("tp")
    x, y, z, c = me // 8, (me // 4) % 2, (me // 2) % 2, me % 2
    return me, 8 - 16 * x, 4 - 8 * y, 2 - 4 * z, 1 - 2 * c


def _greet(peers):
    barrier = pltpu.get_barrier_semaphore()
    for p in peers:
        pl.semaphore_signal(barrier, inc=1, device_id={"tp": p}, device_id_type=MESH)
    pl.semaphore_wait(barrier, len(peers))


def _send(src, dst, send_sem, recv_sem, peer):
    return pltpu.make_async_remote_copy(
        src_ref=src, dst_ref=dst, send_sem=send_sem, recv_sem=recv_sem,
        device_id={"tp": peer}, device_id_type=MESH)


GATHER_SLOTS = 12


def gather_logits(td, x_hbm, lab_ref, w_hbm, xf_hbm, g_hbm, loss_ref,
                  xg, acc, wb, labs, cols, stat, s_out, s_in, gst,
                  send, recv, own_sem, back_sem, w_sem, lab_send, lab_recv, st_send, st_recv, g_sem):
    me, sx, sy, sz, sc = _where_am_i()
    rows, depth = x_hbm.shape
    n = depth // td
    third = rows // 3
    vocab = acc.shape[1]
    core = me % 2
    px, py, pz, pc = me + sx, me + sy, me + sz, me + sc
    _greet((px, py, pz, pc))

    def at(k):
        return pl.ds(pl.multiple_of(k * td, td), td)

    def block(k, dev):
        return xg.at[k % GATHER_SLOTS, dev // 2, dev % 2]

    def copies(k):
        s = k % GATHER_SLOTS

        def copy(i):
            if i < 3:
                src, dst, p = x_hbm.at[:, at(k)], block(k, me), (px, py, pz)[i]
            elif i < 6:
                dev, p = ((px, py), (py, pz), (pz, px))[i - 3]
                src = dst = block(k, dev)
            elif i < 9:
                dev, p = ((px + sy, pz), (py + sz, px), (pz + sx, py))[i - 6]
                src = dst = block(k, dev).at[pl.ds((i - 6) * third, third)]
            else:
                p = pc
                src = dst = xg.at[s, :, core]
            return _send(src, dst, send.at[i, s], recv.at[i, s], p)

        return copy

    def own_copy(k):
        return pltpu.make_async_copy(x_hbm.at[:, at(k)], block(k, me), own_sem.at[k % GATHER_SLOTS])

    def back_copy(k):
        s = k % GATHER_SLOTS
        return pltpu.make_async_copy(xg.at[s], xf_hbm.at[:, :, :, at(k)], back_sem.at[s])

    def w_copy(k):
        rows_k = pl.ds(pl.multiple_of(k * td, td), td)
        return pltpu.make_async_copy(w_hbm.at[rows_k, :], wb.at[k % 2], w_sem.at[k % 2])

    labs[me] = lab_ref[...]

    def lab_copy(i):
        size = 1 << i
        p = (pc, pz, py, px)[i]
        part = labs.at[pl.ds((me // size) * size, size)]
        return _send(part, part, lab_send.at[i], lab_recv.at[i], p)

    w_copy(0).start()
    acc[...] = jnp.zeros_like(acc)

    def step(t, _):
        for i in range(5):
            @pl.when(t == 3 * i + 2)
            def _():
                if i > 0:
                    lab_copy(i - 1).wait()
                if i < 4:
                    lab_copy(i).start()

        k4 = t - 6

        @pl.when((k4 >= 0) & (k4 < n))
        def _():
            cs = copies(k4)
            for i in range(6, 9):
                cs(i).wait_recv()
            own_copy(k4).wait()
            cs(9).start()

        k3 = t - 4

        @pl.when((k3 >= 0) & (k3 < n))
        def _():
            cs = copies(k3)
            for i in range(3, 6):
                cs(i).wait_recv()
            for i in range(6, 9):
                cs(i).start()

        k2 = t - 2

        @pl.when((k2 >= 0) & (k2 < n))
        def _():
            cs = copies(k2)
            for i in range(3):
                cs(i).wait_recv()
            for i in range(3, 6):
                cs(i).start()

        @pl.when(t < n)
        def _():
            cs = copies(t)
            for i in range(3):
                cs(i).start()
            own_copy(t).start()

        k5 = t - 8

        @pl.when((k5 >= 0) & (k5 < n))
        def _():
            cs = copies(k5)
            cs(9).wait_recv()
            w_copy(k5).wait()

            @pl.when(k5 + 1 < n)
            def _():
                w_copy(k5 + 1).start()

            @pl.when(k5 > 0)
            def _():
                back_copy(k5 - 1).wait()

            back_copy(k5).start()
            for i in range(10):
                cs(i).wait_send()
            s, b = k5 % GATHER_SLOTS, k5 % 2
            width = min(512, vocab)

            def part(j, _):
                c = pl.ds(pl.multiple_of(j * width, width), width)
                lhs = xg[s].reshape(16 * rows, td)
                acc[:, c] += jnp.dot(lhs, wb[b, :, c], preferred_element_type=F32)
                return 0

            lax.fori_loop(0, vocab // width, part, 0)

        return 0

    lax.fori_loop(0, max(n + 8, 16), step, 0)
    back_copy(n - 1).wait()

    lane = lax.broadcasted_iota(jnp.int32, (rows, 128), 1)
    column = lax.broadcasted_iota(jnp.int32, (rows, vocab), 1)

    def spread(row):
        return jnp.transpose(jnp.broadcast_to(row, (128, 128)))[:rows]

    def local(d, _):
        z = acc[pl.ds(pl.multiple_of(d * rows, rows), rows), :]
        lab = spread(labs[d][:1]) - me * vocab
        cols[pl.ds(pl.multiple_of(d * rows, rows), rows), :] = lab
        m = jnp.max(z, 1, keepdims=True)
        total = jnp.sum(jnp.exp(z - m), 1, keepdims=True)
        right = jnp.sum(jnp.where(column == lab[:, :1], z, 0.0), 1, keepdims=True)
        t = jnp.where(lane == 0, m, jnp.where(lane == 1, total, right))
        t = jnp.transpose(jnp.concatenate([t, jnp.zeros((128 - rows, 128), F32)], 0))
        for i in range(3):
            stat[i, pl.ds(d, 1), :] = t[i:i + 1]
        return 0

    lax.fori_loop(0, 16, local, 0)
    m, total, right = stat[0], stat[1], stat[2]
    for i, p in enumerate((pc, pz, py, px)):
        s_out[i, 0], s_out[i, 1], s_out[i, 2] = m, total, right
        cp = _send(s_out.at[i], s_in.at[i], st_send.at[i], st_recv.at[i], p)
        cp.start()
        cp.wait()
        m2, total2, right2 = s_in[i, 0], s_in[i, 1], s_in[i, 2]
        top = jnp.maximum(m, m2)
        total = total * jnp.exp(m - top) + total2 * jnp.exp(m2 - top)
        m, right = top, right + right2
    lse = jnp.log(total) + m
    loss_ref[...] = lse - right
    stat[0] = lse

    def g_copy(d):
        return pltpu.make_async_copy(gst.at[pl.ds(pl.multiple_of(d * rows, rows), rows)], g_hbm.at[d // 2, d % 2], g_sem.at[d])

    def grad(d, _):
        r = pl.ds(pl.multiple_of(d * rows, rows), rows)
        l = spread(stat[0, pl.ds(d, 1), :])
        hit = column == cols[r, :][:, :1]
        gst[r, :] = (jnp.exp(acc[r, :] - l[:, :1]) - hit.astype(F32)).astype(BF16)
        g_copy(d).start()
        return 0

    lax.fori_loop(0, 16, grad, 0)
    lax.fori_loop(0, 16, lambda d, _: (g_copy(d).wait(), 0)[1], 0)


def call_gather_logits(x, lab, w, td):
    rows, depth = x.shape
    vocab = w.shape[1]
    s = GATHER_SLOTS
    anywhere, vmem = pl.BlockSpec(memory_space=pl.ANY), pl.BlockSpec(memory_space=pltpu.VMEM)
    return pl.pallas_call(
        functools.partial(gather_logits, td),
        out_shape=(
            jax.ShapeDtypeStruct((8, 2, rows, depth), BF16),
            jax.ShapeDtypeStruct((8, 2, rows, vocab), BF16),
            jax.ShapeDtypeStruct((16, 128), F32),
        ),
        in_specs=[anywhere, vmem, anywhere],
        out_specs=(anywhere, anywhere, vmem),
        scratch_shapes=[
            pltpu.VMEM((s, 8, 2, rows, td), BF16),
            pltpu.VMEM((16 * rows, vocab), F32),
            pltpu.VMEM((2, td, vocab), BF16),
            pltpu.VMEM((16, 8, 128), jnp.int32),
            pltpu.VMEM((16 * rows, 128), jnp.int32),
            pltpu.VMEM((3, 16, 128), F32),
            pltpu.VMEM((4, 3, 16, 128), F32),
            pltpu.VMEM((4, 3, 16, 128), F32),
            pltpu.VMEM((16 * rows, vocab), BF16),
            pltpu.SemaphoreType.DMA((10, s)),
            pltpu.SemaphoreType.DMA((10, s)),
            pltpu.SemaphoreType.DMA((s,)),
            pltpu.SemaphoreType.DMA((s,)),
            pltpu.SemaphoreType.DMA((2,)),
            pltpu.SemaphoreType.DMA((4,)),
            pltpu.SemaphoreType.DMA((4,)),
            pltpu.SemaphoreType.DMA((4,)),
            pltpu.SemaphoreType.DMA((4,)),
            pltpu.SemaphoreType.DMA((16,)),
        ],
        compiler_params=pltpu.CompilerParams(
            collective_id=0, has_side_effects=True, vmem_limit_bytes=60 << 20),
        cost_estimate=pl.CostEstimate(flops=2 * 16 * rows * depth * vocab, bytes_accessed=depth * vocab * 2, transcendentals=0),
        name="gather_logits",
    )(x, lab, w)


SLOTS = 10


def states_grad(td, g_hbm, w_hbm, out_ref, gv, wb, f, s0, r0, s1, r1, s2, r2, s3, r3, g_sem, w_sem, send, recv):
    me, sx, sy, sz, sc = _where_am_i()
    rows = g_hbm.shape[2]
    depth, vocab = w_hbm.shape
    n = depth // td
    third = rows // 3
    core = me % 2
    px, py, pz, pc = me + sx, me + sy, me + sz, me + sc
    chip = me // 2
    cx, cy, cz = sx // 2, sy // 2, sz // 2

    for h, c in enumerate((core, 1 - core)):
        pltpu.make_async_copy(g_hbm.at[:, c], gv.at[h], g_sem.at[h]).start()

    def w_copy(k):
        rows_k = pl.ds(pl.multiple_of(k * td, td), td)
        return pltpu.make_async_copy(w_hbm.at[rows_k, :], wb.at[k % 2], w_sem.at[k % 2])

    w_copy(0).start()
    _greet((px, py, pz, pc))

    def copies(k):
        s = k % SLOTS

        def copy(i):
            if i == 0:
                src, dst, p = s0.at[s], r0.at[s], pc
            elif i < 4:
                src, dst, p = s1.at[s, pl.ds((i - 1) * third, third)], r1.at[s, i - 1], (pz, px, py)[i - 1]
            elif i < 7:
                src, dst, p = s2.at[s, i - 4], r2.at[s, i - 4], (py, pz, px)[i - 4]
            else:
                src, dst, p = s3.at[s, i - 7], r3.at[s, i - 7], (px, py, pz)[i - 7]
            return _send(src, dst, send.at[i, s], recv.at[i, s], p)

        return copy

    def both(s, dest):
        return f[s, dest] + r0[s, dest].astype(F32)

    for h, c in enumerate((core, 1 - core)):
        pltpu.make_async_copy(g_hbm.at[:, c], gv.at[h], g_sem.at[h]).wait()

    def step(t, _):
        ke = t - 7

        @pl.when((ke >= 0) & (ke < n))
        def _():
            s = ke % SLOTS
            cs = copies(ke)
            for i in range(7, 10):
                cs(i).wait_recv()
            total = both(s, chip) + r3[s, 0].astype(F32) + r3[s, 1].astype(F32) + r3[s, 2].astype(F32)
            out_ref[:, pl.ds(pl.multiple_of(ke * td, td), td)] = total.astype(BF16)
            for i in range(10):
                cs(i).wait_send()

        kd = t - 5

        @pl.when((kd >= 0) & (kd < n))
        def _():
            s = kd % SLOTS
            cs = copies(kd)
            for i, dest in enumerate((chip + cx, chip + cy, chip + cz)):
                cs(4 + i).wait_recv()
                s3[s, i] = (both(s, dest) + r2[s, i].astype(F32)).astype(BF16)
                cs(7 + i).start()

        kc = t - 3

        @pl.when((kc >= 0) & (kc < n))
        def _():
            s = kc % SLOTS
            cs = copies(kc)
            for i, dest in enumerate((chip + cx + cy, chip + cy + cz, chip + cz + cx)):
                cs(1 + i).wait_recv()
                total = both(s, dest)
                a, b = i * third, (i + 1) * third
                middle = total[a:b] + r1[s, i].astype(F32)
                if i > 0:
                    s2[s, i, :a] = total[:a].astype(BF16)
                s2[s, i, a:b] = middle.astype(BF16)
                if i < 2:
                    s2[s, i, b:] = total[b:].astype(BF16)
                cs(4 + i).start()

        kb = t - 1

        @pl.when((kb >= 0) & (kb < n))
        def _():
            s = kb % SLOTS
            cs = copies(kb)
            cs(0).wait_recv()
            s1[s] = both(s, chip + cx + cy + cz).astype(BF16)
            for i in range(3):
                cs(1 + i).start()

        @pl.when(t < n)
        def _():
            s, b = t % SLOTS, t % 2
            w_copy(t).wait()

            @pl.when(t + 1 < n)
            def _():
                w_copy(t + 1).start()

            def term(h):
                lhs = gv[h].reshape(8 * rows, vocab)
                return lax.dot_general(lhs, wb[b], (((1,), (1,)), ((), ())), preferred_element_type=F32)

            s0[s] = term(1).astype(BF16).reshape(8, rows, td)
            copies(t)(0).start()
            f[s] = term(0).reshape(8, rows, td)

        return 0

    lax.fori_loop(0, n + 7, step, 0)


def call_states_grad(g, w, td):
    rows, vocab = g.shape[2:]
    depth = w.shape[0]
    s = SLOTS
    anywhere, vmem = pl.BlockSpec(memory_space=pl.ANY), pl.BlockSpec(memory_space=pltpu.VMEM)
    blocks = lambda *shape, dtype=BF16: pltpu.VMEM((*shape, td), dtype)
    return pl.pallas_call(
        functools.partial(states_grad, td),
        out_shape=jax.ShapeDtypeStruct((rows, depth), BF16),
        in_specs=[anywhere, anywhere],
        out_specs=vmem,
        scratch_shapes=[
            pltpu.VMEM((2, 8, rows, vocab), BF16),
            pltpu.VMEM((2, td, vocab), BF16),
            blocks(s, 8, rows, dtype=F32),
            blocks(s, 8, rows),
            blocks(s, 8, rows),
            blocks(s, rows),
            blocks(s, 3, rows // 3),
            blocks(s, 3, rows),
            blocks(s, 3, rows),
            blocks(s, 3, rows),
            blocks(s, 3, rows),
            pltpu.SemaphoreType.DMA((2,)),
            pltpu.SemaphoreType.DMA((2,)),
            pltpu.SemaphoreType.DMA((10, s)),
            pltpu.SemaphoreType.DMA((10, s)),
        ],
        compiler_params=pltpu.CompilerParams(
            collective_id=1, has_side_effects=True, vmem_limit_bytes=67043328),
        cost_estimate=pl.CostEstimate(flops=2 * 16 * rows * depth * vocab, bytes_accessed=depth * vocab * 2, transcendentals=0),
        name="states_grad",
    )(g, w)


def matrix_grad(x_ref, g_ref, out_ref):
    vocab = out_ref.shape[1]
    width = min(512, vocab)

    def part(j, _):
        c = pl.ds(pl.multiple_of(j * width, width), width)
        out_ref[:, c] = lax.dot_general(
            x_ref[...], g_ref[:, c], (((0,), (0,)), ((), ())), preferred_element_type=F32).astype(BF16)
        return 0

    lax.fori_loop(0, vocab // width, part, 0)


def call_matrix_grad(x, g, tile):
    rows, depth = x.shape
    vocab = g.shape[1]
    return pl.pallas_call(
        matrix_grad,
        grid=(depth // tile,),
        out_shape=jax.ShapeDtypeStruct((depth, vocab), BF16),
        in_specs=[pl.BlockSpec((rows, tile), lambda i: (0, i)), pl.BlockSpec((rows, vocab), lambda i: (0, 0))],
        out_specs=pl.BlockSpec((tile, vocab), lambda i: (i, 0)),
        compiler_params=pltpu.CompilerParams(vmem_limit_bytes=48 << 20),
        cost_estimate=pl.CostEstimate(flops=2 * rows * depth * vocab, bytes_accessed=2 * depth * (rows + vocab), transcendentals=0),
        name="matrix_grad",
    )(x, g)


def solution(mesh):
    def step(x, w, label):
        rows, depth = x.shape
        vocab = w.shape[1]
        td = 512 if depth % 512 == 0 and depth > 4096 else 128
        me = lax.axis_index("tp")
        lab = jnp.pad(label[None, :], ((0, 7), (0, 128 - rows)))
        xf, g, loss = call_gather_logits(x, lab, w, td)
        by_x = call_states_grad(g, w, td)
        by_w = call_matrix_grad(xf.reshape(16 * rows, depth), g.reshape(16 * rows, vocab), min(1024, depth))
        return lax.dynamic_slice_in_dim(loss[:, :rows], me, 1)[0], by_x, by_w

    return jax.shard_map(
        step,
        mesh=mesh,
        in_specs=(P(("dp", "tp"), None), P(None, "tp"), P(("dp", "tp"))),
        out_specs=(P(("dp", "tp")), P(("dp", "tp"), None), P("dp", "tp")),
        check_vma=False,
    )
```

time: 574 us -> 413 us (0.72)
  Pallas kernels: 0 us -> 407 us
  matrix products: 279 us -> 0 us
  waiting for transfers between devices: 146 us -> 0 us
  local copies, waits for them, and re-layouts: 67.3 us -> 5.67 us
  blocking collectives: 48.8 us -> 0 us
  other arithmetic: 16.1 us -> 0 us
  between operations: 14.1 us -> 0.65 us
    pallas_call x0 -> x3, Pallas kernels: none -> 407 us  [the longest x1 173 us: call_gather_logits(): pl.pallas_call(functools.partial(gather_logits, td), out_shape=(jax.Shape...]
    dot_general x3 -> x0, matrix products: 279 us -> none  [the longest x1 103 us: step(): jnp.dot(rows.T, by_logits, preferred_element_type=jnp.float32)]
    all_gather x1 -> x0, waiting for transfers between devices: 114 us -> none  [step(): rows = lax.all_gather(x, 'tp', axis=0, tiled=True)]
    unnamed x17 -> x1, local copies, waits for them, and re-layouts: 67.2 us -> 3.22 us
    unnamed x1 -> x0, blocking collectives: 35.3 us -> none
    reduce_scatter x1 -> x0, waiting for transfers between devices: 31.5 us -> none  [step(): by_x = lax.psum_scatter(term, 'tp', scatter_dimension=0, tiled=True)]
    all_gather x1 -> x0, blocking collectives: 13.6 us -> none  [step(): high, sums, right = jnp.moveaxis(lax.all_gather(own, 'tp'), 1, 0)]
    reduce_sum x2 -> x0, other arithmetic: 8.07 us -> none  [the longest x1 8.04 us: step(): jnp.sum(jnp.exp(logits - high[:, None]), -1)]
  transfers between devices with their start and end apart: 2 -> 0, of which waited for: 2 -> 0; matrix products, arithmetic and copies ran while one was open for 30% -> 0% of each run, Pallas kernels for 0% -> 0%
where the time goes in v1:
time: 413 us
  Pallas kernels  407 us (99%)
  local copies, waits for them, and re-layouts  5.67 us (1%)
    pallas_call x1, Pallas kernels, call_gather_logits(): pl.pallas_call(functools.partial(gather_logits, td), out_shape=(jax.Shape...  173 us
    pallas_call x1, Pallas kernels, call_states_grad(): pl.pallas_call(functools.partial(states_grad, td), out_shape=jax.ShapeDty...  140 us
    pallas_call x1, Pallas kernels, call_matrix_grad(): pl.pallas_call(matrix_grad, grid=(depth // tile,), out_shape=jax.ShapeDty...  93.9 us

profile of v1, /device:TPU:0, one launch (start us, length us, event | category | flops | bytes accessed | tf_op | source)
XLA Modules:
  0.0 413.1 jit_solution(14992483026647566884)
XLA Ops:
  0.6 1.3 pad.4.lab_ref
  1.9 173.4 %gather_logits.1 = (bf16[8,2,96,12288]{3,2,1,0:T(8,128)(2,1)}, bf16[8,2,96,2048]{3,2,1,0:T(8,128)(2,1)}, f32[16,128]{1,0:T(8,128)}) custom-call(bf16[96,12288]{1,0:T(8,128)(2,1)} %x_hbm.1, s32[8,128]{1,0:T(8,128)} %pad.4.lab_ref, bf16[12288,2048]{1,0:T(8,128)(2,1)} %w_hbm.3), custom_call_target="tpu_custom_call" | custom-call | flops 77309411328 | bytes 50331648 | tf_op jit(solution)/shard_map/gather_logits/pallas_call | solution.py:230
  175.3 1.2 dynamic-slice_bitcast_fusion
  176.5 93.9 %matrix_grad.1 = bf16[12288,2048]{1,0:T(8,128)(2,1)} custom-call(bf16[1536,12288]{1,0:T(8,128)(2,1)} %bitcast.7, bf16[1536,2048]{1,0:T(8,128)(2,1)} %bitcast.8), custom_call_target="tpu_custom_call" | custom-call | flops 77309411328 | bytes 88080384 | tf_op jit(solution)/shard_map/matrix_grad/pallas_call | solution.py:440
  270.3 139.5 %states_grad.1 = bf16[96,12288]{1,0:T(8,128)(2,1)} custom-call(bf16[8,2,96,2048]{3,2,1,0:T(8,128)(2,1)} %get-tuple-element.7.g_hbm, bf16[12288,2048]{1,0:T(8,128)(2,1)} %w_hbm.3), custom_call_target="tpu_custom_call" | custom-call | flops 77309411328 | bytes 50331648 | tf_op jit(solution)/shard_map/states_grad/pallas_call | solution.py:395
  409.9 3.2 copy.7

commit v2 on v1

v2 whole, which is shorter than its diff:
```python
import functools

import jax
import jax.numpy as jnp
from jax import lax
from jax.experimental import pallas as pl
from jax.experimental.pallas import tpu as pltpu
from jax.sharding import PartitionSpec as P

MESH = pl.DeviceIdType.MESH
F32, BF16 = jnp.float32, jnp.bfloat16


def _where_am_i():
    me = lax.axis_index("tp")
    x, y, z, c = me // 8, (me // 4) % 2, (me // 2) % 2, me % 2
    return me, 8 - 16 * x, 4 - 8 * y, 2 - 4 * z, 1 - 2 * c


def _greet(peers):
    barrier = pltpu.get_barrier_semaphore()
    for p in peers:
        pl.semaphore_signal(barrier, inc=1, device_id={"tp": p}, device_id_type=MESH)
    pl.semaphore_wait(barrier, len(peers))


def _send(src, dst, send_sem, recv_sem, peer):
    return pltpu.make_async_remote_copy(
        src_ref=src, dst_ref=dst, send_sem=send_sem, recv_sem=recv_sem,
        device_id={"tp": peer}, device_id_type=MESH)


GATHER_SLOTS = 12


def gather_logits(td, x_hbm, lab_ref, w_hbm, xf_hbm, g_hbm, loss_ref,
                  xg, acc, wb, labs, cols, stat, scale, s_out, s_in, gst,
                  send, recv, own_sem, back_sem, w_sem, lab_send, lab_recv, st_send, st_recv, g_sem):
    me, sx, sy, sz, sc = _where_am_i()
    rows, depth = x_hbm.shape
    n = depth // td
    third = rows // 3
    vocab = acc.shape[1]
    core = me % 2
    px, py, pz, pc = me + sx, me + sy, me + sz, me + sc
    far = (px, py, pz, px + sy, py + sz, pz + sx, px + sy + sz)
    _greet((*far, pc))

    def at(k):
        return pl.ds(pl.multiple_of(k * td, td), td)

    def block(k, dev):
        return xg.at[k % GATHER_SLOTS, dev // 2, dev % 2]

    def copies(k):
        s = k % GATHER_SLOTS

        def copy(i):
            if i < 3:
                src, dst, p = x_hbm.at[:, at(k)], block(k, me), (px, py, pz)[i]
            elif i < 6:
                dev, p = ((px, py), (py, pz), (pz, px))[i - 3]
                src = dst = block(k, dev)
            elif i < 9:
                dev, p = ((px + sy, pz), (py + sz, px), (pz + sx, py))[i - 6]
                src = dst = block(k, dev).at[pl.ds((i - 6) * third, third)]
            else:
                p = pc
                src = dst = xg.at[s, :, core]
            return _send(src, dst, send.at[i, s], recv.at[i, s], p)

        return copy

    def own_copy(k):
        return pltpu.make_async_copy(x_hbm.at[:, at(k)], block(k, me), own_sem.at[k % GATHER_SLOTS])

    def back_copy(k):
        s = k % GATHER_SLOTS
        return pltpu.make_async_copy(xg.at[s], xf_hbm.at[:, :, :, at(k)], back_sem.at[s])

    def w_copy(k):
        rows_k = pl.ds(pl.multiple_of(k * td, td), td)
        return pltpu.make_async_copy(w_hbm.at[rows_k, :], wb.at[k % 2], w_sem.at[k % 2])

    labs[me] = lab_ref[...]

    def lab_copy(i):
        size = 1 << i
        p = (pc, pz, py, px)[i]
        part = labs.at[pl.ds((me // size) * size, size)]
        return _send(part, part, lab_send.at[i], lab_recv.at[i], p)

    w_copy(0).start()
    acc[...] = jnp.zeros_like(acc)

    def step(t, _):
        for i in range(5):
            @pl.when(t == 3 * i + 2)
            def _():
                if i > 0:
                    lab_copy(i - 1).wait()
                if i < 4:
                    lab_copy(i).start()

        k4 = t - 5

        @pl.when((k4 >= 0) & (k4 < n))
        def _():
            cs = copies(k4)
            for i in range(6, 9):
                cs(i).wait_recv()
            own_copy(k4).wait()
            cs(9).start()

        k3 = t - 4

        @pl.when((k3 >= 0) & (k3 < n))
        def _():
            cs = copies(k3)
            for i in range(3, 6):
                cs(i).wait_recv()
            for i in range(6, 9):
                cs(i).start()

        k2 = t - 2

        @pl.when((k2 >= 0) & (k2 < n))
        def _():
            cs = copies(k2)
            for i in range(3):
                cs(i).wait_recv()
            for i in range(3, 6):
                cs(i).start()

        @pl.when(t < n)
        def _():
            cs = copies(t)
            for i in range(3):
                cs(i).start()
            own_copy(t).start()

        k5 = t - 6

        @pl.when((k5 >= 0) & (k5 < n))
        def _():
            cs = copies(k5)
            cs(9).wait_recv()
            w_copy(k5).wait()

            @pl.when(k5 + 1 < n)
            def _():
                w_copy(k5 + 1).start()

            @pl.when(k5 > 0)
            def _():
                back_copy(k5 - 1).wait()

            back_copy(k5).start()
            for i in range(10):
                cs(i).wait_send()
            lhs = xg[k5 % GATHER_SLOTS].reshape(16 * rows, td)
            acc[...] += jnp.dot(lhs, wb[k5 % 2], preferred_element_type=F32)

        return 0

    lax.fori_loop(0, max(n + 6, 16), step, 0)
    back_copy(n - 1).wait()

    lane = lax.broadcasted_iota(jnp.int32, (rows, 128), 1)
    parts = [pl.ds(i * 128, 128) for i in range(vocab // 128)]

    def rows_of(d):
        return pl.ds(pl.multiple_of(d * rows, rows), rows)

    def spread(row):
        return jnp.transpose(jnp.broadcast_to(row, (128, 128)))[:rows]

    def local(h, d, _):
        r = rows_of(d)
        lab = spread(labs[d][:1]) - me * vocab
        cols[r, :] = lab
        m = acc[r, parts[0]]
        for p in parts[1:]:
            m = jnp.maximum(m, acc[r, p])
        m = jnp.max(m, 1, keepdims=True)
        total = right = jnp.zeros((rows, 128), F32)
        for i, p in enumerate(parts):
            z = acc[r, p]
            right += jnp.where(lane + i * 128 == lab, z, 0.0)
            e = jnp.exp(z - m)
            acc[r, p] = e
            total += e
        total, right = jnp.sum(total, 1, keepdims=True), jnp.sum(right, 1, keepdims=True)
        t = jnp.where(lane == 0, m, jnp.where(lane == 1, total, right))
        t = jnp.transpose(jnp.concatenate([t, jnp.zeros((128 - rows, 128), F32)], 0))
        for i in range(3):
            stat[h, i, pl.ds(d - 8 * h, 1), :] = t[i:i + 1]
        scale[h, pl.ds(d - 8 * h, 1), :] = t[:1]
        return 0

    def near_copy(h):
        return _send(s_out.at[h, 0], s_in.at[h, 0], st_send.at[h, 0], st_recv.at[h, 0], pc)

    def far_copy(h, i):
        return _send(s_out.at[h, 1], s_in.at[h, i + 1], st_send.at[h, i + 1], st_recv.at[h, i + 1], far[i])

    def merge(a, b):
        top = jnp.maximum(a[0], b[0])
        return top, a[1] * jnp.exp(a[0] - top) + b[1] * jnp.exp(b[0] - top), a[2] + b[2]

    def figures(ref):
        return ref[0], ref[1], ref[2]

    def start_near(h):
        s_out[h, 0] = stat[h]
        near_copy(h).start()

    def start_far(h):
        near_copy(h).wait()
        for i, a in enumerate(merge(figures(stat.at[h]), figures(s_in.at[h, 0]))):
            s_out[h, 1, i] = a
        for i in range(7):
            far_copy(h, i).start()

    def end_far(h):
        for i in range(7):
            far_copy(h, i).wait()
        a = [figures(s_out.at[h, 1])] + [figures(s_in.at[h, i + 1]) for i in range(7)]
        while len(a) > 1:
            a = [merge(*p) for p in zip(a[::2], a[1::2])]
        lse = jnp.log(a[0][1]) + a[0][0]
        loss_ref[pl.ds(8 * h, 8), :] = lse - a[0][2]
        scale[h] = jnp.exp(scale[h] - lse)

    def g_copy(d):
        return pltpu.make_async_copy(gst.at[rows_of(d)], g_hbm.at[d // 2, d % 2], g_sem.at[d])

    def grad(h, d, _):
        r = rows_of(d)
        f = spread(scale[h, pl.ds(d - 8 * h, 1), :])
        lab = cols[r, :]
        for i, p in enumerate(parts):
            gst[r, p] = (acc[r, p] * f - jnp.where(lane + i * 128 == lab, 1.0, 0.0)).astype(BF16)
        g_copy(d).start()
        return 0

    lax.fori_loop(0, 8, functools.partial(local, 0), 0)
    start_near(0)
    lax.fori_loop(8, 10, functools.partial(local, 1), 0)
    start_far(0)
    lax.fori_loop(10, 16, functools.partial(local, 1), 0)
    start_near(1)
    end_far(0)
    lax.fori_loop(0, 4, functools.partial(grad, 0), 0)
    start_far(1)
    lax.fori_loop(4, 8, functools.partial(grad, 0), 0)
    end_far(1)
    lax.fori_loop(8, 16, functools.partial(grad, 1), 0)
    lax.fori_loop(0, 16, lambda d, _: (g_copy(d).wait(), 0)[1], 0)


def call_gather_logits(x, lab, w, td):
    rows, depth = x.shape
    vocab = w.shape[1]
    s = GATHER_SLOTS
    anywhere, vmem = pl.BlockSpec(memory_space=pl.ANY), pl.BlockSpec(memory_space=pltpu.VMEM)
    return pl.pallas_call(
        functools.partial(gather_logits, td),
        out_shape=(
            jax.ShapeDtypeStruct((8, 2, rows, depth), BF16),
            jax.ShapeDtypeStruct((8, 2, rows, vocab), BF16),
            jax.ShapeDtypeStruct((16, 128), F32),
        ),
        in_specs=[anywhere, vmem, anywhere],
        out_specs=(anywhere, anywhere, vmem),
        scratch_shapes=[
            pltpu.VMEM((s, 8, 2, rows, td), BF16),
            pltpu.VMEM((16 * rows, vocab), F32),
            pltpu.VMEM((2, td, vocab), BF16),
            pltpu.VMEM((16, 8, 128), jnp.int32),
            pltpu.VMEM((16 * rows, 128), jnp.int32),
            pltpu.VMEM((2, 3, 8, 128), F32),
            pltpu.VMEM((2, 8, 128), F32),
            pltpu.VMEM((2, 2, 3, 8, 128), F32),
            pltpu.VMEM((2, 8, 3, 8, 128), F32),
            pltpu.VMEM((16 * rows, vocab), BF16),
            pltpu.SemaphoreType.DMA((10, s)),
            pltpu.SemaphoreType.DMA((10, s)),
            pltpu.SemaphoreType.DMA((s,)),
            pltpu.SemaphoreType.DMA((s,)),
            pltpu.SemaphoreType.DMA((2,)),
            pltpu.SemaphoreType.DMA((4,)),
            pltpu.SemaphoreType.DMA((4,)),
            pltpu.SemaphoreType.DMA((2, 8)),
            pltpu.SemaphoreType.DMA((2, 8)),
            pltpu.SemaphoreType.DMA((16,)),
        ],
        compiler_params=pltpu.CompilerParams(
            collective_id=0, has_side_effects=True, vmem_limit_bytes=67043328),
        cost_estimate=pl.CostEstimate(flops=2 * 16 * rows * depth * vocab, bytes_accessed=depth * vocab * 2, transcendentals=0),
        name="gather_logits",
    )(x, lab, w)


SLOTS = 8


def states_grad(td, early, g_hbm, w_hbm, xf_hbm, out_ref, dw_hbm, gv, wb, xt, dwb, f, s0, r0, s1, r1, s2, r2, s3, r3,
                g_sem, w_sem, x_sem, dw_sem, send, recv):
    me, sx, sy, sz, sc = _where_am_i()
    rows = g_hbm.shape[2]
    depth, vocab = w_hbm.shape
    n = depth // td
    third = rows // 3
    core = me % 2
    px, py, pz, pc = me + sx, me + sy, me + sz, me + sc
    chip = me // 2
    cx, cy, cz = sx // 2, sy // 2, sz // 2

    for h, c in enumerate((core, 1 - core)):
        pltpu.make_async_copy(g_hbm.at[:, c], gv.at[h], g_sem.at[h]).start()

    def w_copy(k):
        rows_k = pl.ds(pl.multiple_of(k * td, td), td)
        return pltpu.make_async_copy(w_hbm.at[rows_k, :], wb.at[k % 2], w_sem.at[k % 2])

    def x_copy(k, h):
        c = core if h == 0 else 1 - core
        cols = pl.ds(pl.multiple_of(k * td, td), td)
        return pltpu.make_async_copy(xf_hbm.at[:, c, :, cols], xt.at[k % 2, h], x_sem.at[k % 2, h])

    def dw_copy(k):
        rows_k = pl.ds(pl.multiple_of(k * td, td), td)
        return pltpu.make_async_copy(dwb.at[k % 2], dw_hbm.at[rows_k, :], dw_sem.at[k % 2])

    w_copy(0).start()
    for h in range(2):
        x_copy(0, h).start()
    _greet((px, py, pz, pc))

    def copies(k):
        s = k % SLOTS

        def copy(i):
            if i == 0:
                src, dst, p = s0.at[s], r0.at[s], pc
            elif i < 4:
                src, dst, p = s1.at[s, pl.ds((i - 1) * third, third)], r1.at[s, i - 1], (pz, px, py)[i - 1]
            elif i < 7:
                src, dst, p = s2.at[s, i - 4], r2.at[s, i - 4], (py, pz, px)[i - 4]
            else:
                src, dst, p = s3.at[s, i - 7], r3.at[s, i - 7], (px, py, pz)[i - 7]
            return _send(src, dst, send.at[i, s], recv.at[i, s], p)

        return copy

    def both(s, dest):
        return f[s, dest] + r0[s, dest].astype(F32)

    for h, c in enumerate((core, 1 - core)):
        pltpu.make_async_copy(g_hbm.at[:, c], gv.at[h], g_sem.at[h]).wait()

    stages = ((1, range(0, 1), range(1, 4)), (2, range(1, 4), range(4, 7)), (4, range(4, 7), range(7, 10)), (6, range(7, 10), ()))

    def receive(lag, k):
        for i in stages[lag][1]:
            copies(k)(i).wait_recv()

    def add(lag, k):
        s = k % SLOTS
        if lag == 0:
            s1[s] = both(s, chip + cx + cy + cz).astype(BF16)
        elif lag == 1:
            for i, dest in enumerate((chip + cx + cy, chip + cy + cz, chip + cz + cx)):
                total = both(s, dest)
                a, b = i * third, (i + 1) * third
                if i > 0:
                    s2[s, i, :a] = total[:a].astype(BF16)
                s2[s, i, a:b] = (total[a:b] + r1[s, i].astype(F32)).astype(BF16)
                if i < 2:
                    s2[s, i, b:] = total[b:].astype(BF16)
        elif lag == 2:
            for i, dest in enumerate((chip + cx, chip + cy, chip + cz)):
                s3[s, i] = (both(s, dest) + r2[s, i].astype(F32)).astype(BF16)
        else:
            total = both(s, chip) + r3[s, 0].astype(F32) + r3[s, 1].astype(F32) + r3[s, 2].astype(F32)
            out_ref[:, pl.ds(pl.multiple_of(k * td, td), td)] = total.astype(BF16)

    def forward(lag, k):
        for i in stages[lag][2]:
            copies(k)(i).start()
        if lag == 3:
            for i in range(10):
                copies(k)(i).wait_send()

    def term(h, t):
        lhs = gv[h].reshape(8 * rows, vocab)
        return lax.dot_general(
            lhs, wb[t % 2], (((1,), (1,)), ((), ())), preferred_element_type=F32).reshape(8, rows, td)

    def fetch(t):
        w_copy(t).wait()

        @pl.when(t + 1 < n)
        def _():
            w_copy(t + 1).start()

    def edge(t, _):
        for lag in range(4):
            k = t - stages[lag][0]

            @pl.when((k >= 0) & (k < n))
            def _():
                receive(lag, k)
                add(lag, k)
                forward(lag, k)

        @pl.when(t < n)
        def _():
            fetch(t)
            s0[t % SLOTS] = term(1, t).astype(BF16)
            copies(t)(0).start()
            f[t % SLOTS] = term(0, t)

        matrix_tile(t)
        return 0

    def steady(t, _):
        fetch(t)
        for lag in range(4):
            receive(lag, t - stages[lag][0])
        for lag in range(4):
            add(lag, t - stages[lag][0])
        for lag in range(4):
            forward(lag, t - stages[lag][0])
        s0[t % SLOTS] = term(1, t).astype(BF16)
        copies(t)(0).start()
        f[t % SLOTS] = term(0, t)
        matrix_tile(t)
        return 0

    def matrix_tile(t):
        ki = jnp.where(t < n, t // 3, n // 3 + t - n)

        @pl.when((ki < early) & ((t % 3 == 2) | (t >= n)))
        def _():
            b = ki % 2
            for h in range(2):
                x_copy(ki, h).wait()

            @pl.when(ki + 1 < early)
            def _():
                for h in range(2):
                    x_copy(ki + 1, h).start()

            @pl.when(ki >= 2)
            def _():
                dw_copy(ki - 2).wait()

            dwb[b] = lax.dot_general(
                xt[b].reshape(16 * rows, td), gv[...].reshape(16 * rows, vocab), (((0,), (0,)), ((), ())),
                preferred_element_type=F32).astype(BF16)
            dw_copy(ki).start()

    lax.fori_loop(0, 6, edge, 0)
    lax.fori_loop(6, n, steady, 0)
    lax.fori_loop(n, n + 6, edge, 0)
    for k in (early - 2, early - 1):
        dw_copy(k).wait()


def call_states_grad(g, w, xf, td, early):
    rows, vocab = g.shape[2:]
    depth = w.shape[0]
    s = SLOTS
    anywhere, vmem = pl.BlockSpec(memory_space=pl.ANY), pl.BlockSpec(memory_space=pltpu.VMEM)
    blocks = lambda *shape, dtype=BF16: pltpu.VMEM((*shape, td), dtype)
    return pl.pallas_call(
        functools.partial(states_grad, td, early),
        out_shape=(jax.ShapeDtypeStruct((rows, depth), BF16), jax.ShapeDtypeStruct((early * td, vocab), BF16)),
        in_specs=[anywhere, anywhere, anywhere],
        out_specs=(vmem, anywhere),
        scratch_shapes=[
            pltpu.VMEM((2, 8, rows, vocab), BF16),
            pltpu.VMEM((2, td, vocab), BF16),
            blocks(2, 2, 8, rows),
            pltpu.VMEM((2, td, vocab), BF16),
            blocks(s, 8, rows, dtype=F32),
            blocks(s, 8, rows),
            blocks(s, 8, rows),
            blocks(s, rows),
            blocks(s, 3, rows // 3),
            blocks(s, 3, rows),
            blocks(s, 3, rows),
            blocks(s, 3, rows),
            blocks(s, 3, rows),
            pltpu.SemaphoreType.DMA((2,)),
            pltpu.SemaphoreType.DMA((2,)),
            pltpu.SemaphoreType.DMA((2, 2)),
            pltpu.SemaphoreType.DMA((2,)),
            pltpu.SemaphoreType.DMA((10, s)),
            pltpu.SemaphoreType.DMA((10, s)),
        ],
        compiler_params=pltpu.CompilerParams(
            collective_id=1, has_side_effects=True, vmem_limit_bytes=67043328),
        cost_estimate=pl.CostEstimate(flops=2 * 16 * rows * depth * vocab, bytes_accessed=depth * vocab * 2, transcendentals=0),
        name="states_grad",
    )(g, w, xf)


def matrix_grad(early, x_ref, g_ref, dw_hbm, out_hbm, made, kept, made_sem, in_sem, kept_sem):
    i, n = pl.program_id(0), pl.num_programs(0)
    tile = x_ref.shape[1]

    def at(k):
        return pl.ds(pl.multiple_of(k * tile, tile), tile)

    def made_out(k):
        return pltpu.make_async_copy(made.at[k % 2], out_hbm.at[at(early + k), :], made_sem.at[k % 2])

    def kept_in(k):
        return pltpu.make_async_copy(dw_hbm.at[at(k), :], kept.at[k % 3], in_sem.at[k % 3])

    def kept_out(k):
        return pltpu.make_async_copy(kept.at[k % 3], out_hbm.at[at(k), :], kept_sem.at[k % 3])

    @pl.when(i == 0)
    def _():
        kept_in(0).start()

    @pl.when(i >= 2)
    def _():
        kept_out(i - 2).wait()
        made_out(i - 2).wait()

    @pl.when(i + 1 < n)
    def _():
        kept_in(i + 1).start()

    kept_in(i).wait()
    kept_out(i).start()
    made[i % 2] = lax.dot_general(
        x_ref[...], g_ref[...], (((0,), (0,)), ((), ())), preferred_element_type=F32).astype(BF16)
    made_out(i).start()

    @pl.when(i == n - 1)
    def _():
        for k in (n - 2, n - 1):
            kept_out(k).wait()
            made_out(k).wait()


def call_matrix_grad(x, g, dw, tile):
    rows, depth = x.shape
    vocab = g.shape[1]
    early = dw.shape[0] // tile
    anywhere = pl.BlockSpec(memory_space=pl.ANY)
    return pl.pallas_call(
        functools.partial(matrix_grad, early),
        grid=(depth // tile - early,),
        out_shape=jax.ShapeDtypeStruct((depth, vocab), BF16),
        in_specs=[pl.BlockSpec((rows, tile), lambda i: (0, early + i)), pl.BlockSpec((rows, vocab), lambda i: (0, 0)), anywhere],
        out_specs=anywhere,
        scratch_shapes=[
            pltpu.VMEM((2, tile, vocab), BF16),
            pltpu.VMEM((3, tile, vocab), BF16),
            pltpu.SemaphoreType.DMA((2,)),
            pltpu.SemaphoreType.DMA((3,)),
            pltpu.SemaphoreType.DMA((3,)),
        ],
        compiler_params=pltpu.CompilerParams(vmem_limit_bytes=60 << 20),
        cost_estimate=pl.CostEstimate(flops=rows * depth * vocab, bytes_accessed=2 * depth * (rows + vocab), transcendentals=0),
        name="matrix_grad",
    )(x, g, dw)


def solution(mesh):
    def step(x, w, label):
        rows, depth = x.shape
        vocab = w.shape[1]
        td = 512 if depth % 512 == 0 and depth > 4096 else 128
        me = lax.axis_index("tp")
        lab = jnp.pad(label[None, :], ((0, 7), (0, 128 - rows)))
        xf, g, loss = call_gather_logits(x, lab, w, td)
        by_x, part = call_states_grad(g, w, xf, td, depth // td // 2)
        by_w = call_matrix_grad(xf.reshape(16 * rows, depth), g.reshape(16 * rows, vocab), part, td)
        return lax.dynamic_slice_in_dim(loss[:, :rows], me, 1)[0], by_x, by_w

    return jax.shard_map(
        step,
        mesh=mesh,
        in_specs=(P(("dp", "tp"), None), P(None, "tp"), P(("dp", "tp"))),
        out_specs=(P(("dp", "tp")), P(("dp", "tp"), None), P("dp", "tp")),
        check_vma=False,
    )
```

time: 413 us -> 361 us (0.87)
  Pallas kernels: 407 us -> 356 us
    pallas_call x2, Pallas kernels: 233 us -> 198 us  [the longest x1 149 us: call_states_grad(): pl.pallas_call(functools.partial(states_grad, td, early), out_shape=(jax....]
    pallas_call x1, Pallas kernels: 173 us -> 158 us  [call_gather_logits(): pl.pallas_call(functools.partial(gather_logits, td), out_shape=(jax.Shape...]
where the time goes in v2:
time: 361 us; the launch traced here: 360 us
  Pallas kernels  356 us (99%)
  local copies, waits for them, and re-layouts  3.87 us (1%)
    pallas_call x1, Pallas kernels, call_gather_logits(): pl.pallas_call(functools.partial(gather_logits, td), out_shape=(jax.Shape...  158 us
    pallas_call x1, Pallas kernels, call_states_grad(): pl.pallas_call(functools.partial(states_grad, td, early), out_shape=(jax....  149 us
    pallas_call x1, Pallas kernels, call_matrix_grad(): pl.pallas_call(functools.partial(matrix_grad, early), grid=(depth // tile...  48.7 us

profile of v2, /device:TPU:0, one launch (start us, length us, event | category | flops | bytes accessed | tf_op | source)
XLA Modules:
  0.0 360.3 jit_solution(2853539680810515408)
XLA Ops:
  0.6 1.3 pad.4.lab_ref
  1.9 158.2 %gather_logits.1 = (bf16[8,2,96,12288]{3,2,1,0:T(8,128)(2,1)}, bf16[8,2,96,2048]{3,2,1,0:T(8,128)(2,1)}, f32[16,128]{1,0:T(8,128)}) custom-call(bf16[96,12288]{1,0:T(8,128)(2,1)} %x_hbm.1, s32[8,128]{1,0:T(8,128)} %pad.4.lab_ref, bf16[12288,2048]{1,0:T(8,128)(2,1)} %w_hbm.3), custom_call_target="tpu_custom_call" | custom-call | flops 77309411328 | bytes 50331648 | tf_op jit(solution)/shard_map/gather_logits/pallas_call | solution.py:267
  160.1 1.2 dynamic-slice_bitcast_fusion
  161.3 148.8 %states_grad.1 = (bf16[96,12288]{1,0:T(8,128)(2,1)}, bf16[6144,2048]{1,0:T(8,128)(2,1)}) custom-call(bf16[8,2,96,2048]{3,2,1,0:T(8,128)(2,1)} %get-tuple-element.9.g_hbm, bf16[12288,2048]{1,0:T(8,128)(2,1)} %w_hbm.3, bf16[8,2,96,12288]{3,2,1,0:T(8,128)(2,1)} %get-tuple-element.10.xf_hbm), custom_call_target="tpu_custom_call" | custom-call | flops 77309411328 | bytes 50331648 | tf_op jit(solution)/shard_map/states_grad/pallas_call | solution.py:478
  310.2 0.0 copy-start
  310.2 48.7 %matrix_grad.1 = bf16[12288,2048]{1,0:T(8,128)(2,1)} custom-call(bf16[1536,12288]{1,0:T(8,128)(2,1)} %bitcast.7, bf16[1536,2048]{1,0:T(8,128)(2,1)} %bitcast.8, bf16[6144,2048]{1,0:T(8,128)(2,1)} %get-tuple-element.12.dw_hbm), custom_call_target="tpu_custom_call" | custom-call | flops 38654705664 | bytes 88080384 | tf_op jit(solution)/shard_map/matrix_grad/pallas_call | solution.py:558
  358.9 0.0 copy-done
  358.9 1.4 copy.7
Async XLA Ops:
  310.2 48.7 %copy-start = (bf16[96,12288]{1,0:T(8,128)(2,1)S(1)}, bf16[96,12288]{1,0:T(8,128)(2,1)}, u32[]{:S(2)}) copy-start(bf16[96,12288]{1,0:T(8,128)(2,1)} %get-tuple-element.17) | copy-start | bytes 7077892

commit v3 on v2

--- a/solution.py
+++ b/solution.py
@@ -82,7 +82,7 @@
         rows_k = pl.ds(pl.multiple_of(k * td, td), td)
         return pltpu.make_async_copy(w_hbm.at[rows_k, :], wb.at[k % 2], w_sem.at[k % 2])
 
-    labs[me] = lab_ref[...]
+    labs[me, :1, :rows] = lab_ref[...]
 
     def lab_copy(i):
         size = 1 << i
@@ -91,7 +91,6 @@
         return _send(part, part, lab_send.at[i], lab_recv.at[i], p)
 
     w_copy(0).start()
-    acc[...] = jnp.zeros_like(acc)
 
     def step(t, _):
         for i in range(5):
@@ -102,7 +101,7 @@
                 if i < 4:
                     lab_copy(i).start()
 
-        k4 = t - 5
+        k4 = t - 4
 
         @pl.when((k4 >= 0) & (k4 < n))
         def _():
@@ -112,7 +111,7 @@
             own_copy(k4).wait()
             cs(9).start()
 
-        k3 = t - 4
+        k3 = t - 3
 
         @pl.when((k3 >= 0) & (k3 < n))
         def _():
@@ -139,7 +138,11 @@
                 cs(i).start()
             own_copy(t).start()
 
-        k5 = t - 6
+        @pl.when(t == 1)
+        def _():
+            acc[...] = jnp.zeros_like(acc)
+
+        k5 = t - 5
 
         @pl.when((k5 >= 0) & (k5 < n))
         def _():
@@ -163,7 +166,7 @@
 
         return 0
 
-    lax.fori_loop(0, max(n + 6, 16), step, 0)
+    lax.fori_loop(0, max(n + 5, 16), step, 0)
     back_copy(n - 1).wait()
 
     lane = lax.broadcasted_iota(jnp.int32, (rows, 128), 1)
@@ -175,27 +178,32 @@
     def spread(row):
         return jnp.transpose(jnp.broadcast_to(row, (128, 128)))[:rows]
 
-    def local(h, d, _):
-        r = rows_of(d)
-        lab = spread(labs[d][:1]) - me * vocab
-        cols[r, :] = lab
-        m = acc[r, parts[0]]
-        for p in parts[1:]:
-            m = jnp.maximum(m, acc[r, p])
-        m = jnp.max(m, 1, keepdims=True)
-        total = right = jnp.zeros((rows, 128), F32)
-        for i, p in enumerate(parts):
-            z = acc[r, p]
-            right += jnp.where(lane + i * 128 == lab, z, 0.0)
-            e = jnp.exp(z - m)
-            acc[r, p] = e
-            total += e
-        total, right = jnp.sum(total, 1, keepdims=True), jnp.sum(right, 1, keepdims=True)
-        t = jnp.where(lane == 0, m, jnp.where(lane == 1, total, right))
-        t = jnp.transpose(jnp.concatenate([t, jnp.zeros((128 - rows, 128), F32)], 0))
-        for i in range(3):
-            stat[h, i, pl.ds(d - 8 * h, 1), :] = t[i:i + 1]
-        scale[h, pl.ds(d - 8 * h, 1), :] = t[:1]
+    def local(h, pair, _):
+        ds = (2 * pair, 2 * pair + 1)
+        labels, tops, sums = [], [], []
+        for d in ds:
+            labels.append(spread(labs[d][:1]) - me * vocab)
+            m = acc[rows_of(d), parts[0]]
+            for p in parts[1:]:
+                m = jnp.maximum(m, acc[rows_of(d), p])
+            tops.append(jnp.max(m, 1, keepdims=True))
+        for d, lab, m in zip(ds, labels, tops):
+            cols[rows_of(d), :] = lab
+            total = right = jnp.zeros((rows, 128), F32)
+            for i, p in enumerate(parts):
+                z = acc[rows_of(d), p]
+                right += jnp.where(lane + i * 128 == lab, z, 0.0)
+                e = jnp.exp(z - m)
+                acc[rows_of(d), p] = e
+                total += e
+            sums.append((total, right))
+        for d, m, (total, right) in zip(ds, tops, sums):
+            total, right = jnp.sum(total, 1, keepdims=True), jnp.sum(right, 1, keepdims=True)
+            t = jnp.where(lane == 0, m, jnp.where(lane == 1, total, right))
+            t = jnp.transpose(jnp.concatenate([t, jnp.zeros((128 - rows, 128), F32)], 0))
+            for i in range(3):
+                stat[h, i, pl.ds(d - 8 * h, 1), :] = t[i:i + 1]
+            scale[h, pl.ds(d - 8 * h, 1), :] = t[:1]
         return 0
 
     def near_copy(h):
@@ -235,27 +243,29 @@
     def g_copy(d):
         return pltpu.make_async_copy(gst.at[rows_of(d)], g_hbm.at[d // 2, d % 2], g_sem.at[d])
 
-    def grad(h, d, _):
-        r = rows_of(d)
-        f = spread(scale[h, pl.ds(d - 8 * h, 1), :])
-        lab = cols[r, :]
-        for i, p in enumerate(parts):
-            gst[r, p] = (acc[r, p] * f - jnp.where(lane + i * 128 == lab, 1.0, 0.0)).astype(BF16)
-        g_copy(d).start()
+    def grad(h, pair, _):
+        ds = (2 * pair, 2 * pair + 1)
+        factors = [spread(scale[h, pl.ds(d - 8 * h, 1), :]) for d in ds]
+        for d, f in zip(ds, factors):
+            lab = cols[rows_of(d), :]
+            for i, p in enumerate(parts):
+                g = acc[rows_of(d), p] * f - jnp.where(lane + i * 128 == lab, 1.0, 0.0)
+                gst[rows_of(d), p] = g.astype(BF16)
+            g_copy(d).start()
         return 0
 
-    lax.fori_loop(0, 8, functools.partial(local, 0), 0)
+    lax.fori_loop(0, 4, functools.partial(local, 0), 0)
     start_near(0)
-    lax.fori_loop(8, 10, functools.partial(local, 1), 0)
+    lax.fori_loop(4, 5, functools.partial(local, 1), 0)
     start_far(0)
-    lax.fori_loop(10, 16, functools.partial(local, 1), 0)
+    lax.fori_loop(5, 8, functools.partial(local, 1), 0)
     start_near(1)
     end_far(0)
-    lax.fori_loop(0, 4, functools.partial(grad, 0), 0)
+    lax.fori_loop(0, 2, functools.partial(grad, 0), 0)
     start_far(1)
-    lax.fori_loop(4, 8, functools.partial(grad, 0), 0)
+    lax.fori_loop(2, 4, functools.partial(grad, 0), 0)
     end_far(1)
-    lax.fori_loop(8, 16, functools.partial(grad, 1), 0)
+    lax.fori_loop(4, 8, functools.partial(grad, 1), 0)
     lax.fori_loop(0, 16, lambda d, _: (g_copy(d).wait(), 0)[1], 0)
 
 
@@ -317,8 +327,10 @@
     chip = me // 2
     cx, cy, cz = sx // 2, sy // 2, sz // 2
 
-    for h, c in enumerate((core, 1 - core)):
-        pltpu.make_async_copy(g_hbm.at[:, c], gv.at[h], g_sem.at[h]).start()
+    def g_copy(h):
+        return pltpu.make_async_copy(g_hbm.at[:, core if h == 0 else 1 - core], gv.at[h], g_sem.at[h])
+
+    g_copy(1).start()
 
     def w_copy(k):
         rows_k = pl.ds(pl.multiple_of(k * td, td), td)
@@ -334,6 +346,7 @@
         return pltpu.make_async_copy(dwb.at[k % 2], dw_hbm.at[rows_k, :], dw_sem.at[k % 2])
 
     w_copy(0).start()
+    g_copy(0).start()
     for h in range(2):
         x_copy(0, h).start()
     _greet((px, py, pz, pc))
@@ -357,8 +370,7 @@
     def both(s, dest):
         return f[s, dest] + r0[s, dest].astype(F32)
 
-    for h, c in enumerate((core, 1 - core)):
-        pltpu.make_async_copy(g_hbm.at[:, c], gv.at[h], g_sem.at[h]).wait()
+    g_copy(1).wait()
 
     stages = ((1, range(0, 1), range(1, 4)), (2, range(1, 4), range(4, 7)), (4, range(4, 7), range(7, 10)), (6, range(7, 10), ()))
 
@@ -420,6 +432,11 @@
             fetch(t)
             s0[t % SLOTS] = term(1, t).astype(BF16)
             copies(t)(0).start()
+
+            @pl.when(t == 0)
+            def _():
+                g_copy(0).wait()
+
             f[t % SLOTS] = term(0, t)
 
         matrix_tile(t)
@@ -580,7 +597,7 @@
         vocab = w.shape[1]
         td = 512 if depth % 512 == 0 and depth > 4096 else 128
         me = lax.axis_index("tp")
-        lab = jnp.pad(label[None, :], ((0, 7), (0, 128 - rows)))
+        lab = label.reshape(1, rows)
         xf, g, loss = call_gather_logits(x, lab, w, td)
         by_x, part = call_states_grad(g, w, xf, td, depth // td // 2)
         by_w = call_matrix_grad(xf.reshape(16 * rows, depth), g.reshape(16 * rows, vocab), part, td)

time: 361 us -> 356 us (0.986)
  no operation moved by 1% of the time
where the time goes in v3:
time: 356 us
  Pallas kernels  353 us (99%)
    pallas_call x1, Pallas kernels, call_gather_logits(): pl.pallas_call(functools.partial(gather_logits, td), out_shape=(jax.Shape...  156 us
    pallas_call x1, Pallas kernels, call_states_grad(): pl.pallas_call(functools.partial(states_grad, td, early), out_shape=(jax....  148 us
    pallas_call x1, Pallas kernels, call_matrix_grad(): pl.pallas_call(functools.partial(matrix_grad, early), grid=(depth // tile...  48.7 us

profile of v3, /device:TPU:0, one launch (start us, length us, event | category | flops | bytes accessed | tf_op | source)
XLA Modules:
  0.0 356.0 jit_solution(11867530865655477684)
XLA Ops:
  0.6 156.3 %gather_logits.1 = (bf16[8,2,96,12288]{3,2,1,0:T(8,128)(2,1)}, bf16[8,2,96,2048]{3,2,1,0:T(8,128)(2,1)}, f32[16,128]{1,0:T(8,128)}) custom-call(bf16[96,12288]{1,0:T(8,128)(2,1)} %x_hbm.1, s32[1,96]{1,0:T(1,128)} %bitcast.6, bf16[12288,2048]{1,0:T(8,128)(2,1)} %w_hbm.3), custom_call_target="tpu_custom_call" | custom-call | flops 77309411328 | bytes 50331648 | tf_op jit(solution)/shard_map/gather_logits/pallas_call | solution.py:277
  157.0 1.2 dynamic-slice_bitcast_fusion
  158.2 147.6 %states_grad.1 = (bf16[96,12288]{1,0:T(8,128)(2,1)}, bf16[6144,2048]{1,0:T(8,128)(2,1)}) custom-call(bf16[8,2,96,2048]{3,2,1,0:T(8,128)(2,1)} %get-tuple-element.9.g_hbm, bf16[12288,2048]{1,0:T(8,128)(2,1)} %w_hbm.3, bf16[8,2,96,12288]{3,2,1,0:T(8,128)(2,1)} %get-tuple-element.10.xf_hbm), custom_call_target="tpu_custom_call" | custom-call | flops 77309411328 | bytes 50331648 | tf_op jit(solution)/shard_map/states_grad/pallas_call | solution.py:495
  305.8 0.0 copy-start
  305.8 48.7 %matrix_grad.1 = bf16[12288,2048]{1,0:T(8,128)(2,1)} custom-call(bf16[1536,12288]{1,0:T(8,128)(2,1)} %bitcast.7, bf16[1536,2048]{1,0:T(8,128)(2,1)} %bitcast.8, bf16[6144,2048]{1,0:T(8,128)(2,1)} %get-tuple-element.12.dw_hbm), custom_call_target="tpu_custom_call" | custom-call | flops 38654705664 | bytes 88080384 | tf_op jit(solution)/shard_map/matrix_grad/pallas_call | solution.py:575
  354.6 0.0 copy-done
  354.6 1.4 copy.7
Async XLA Ops:
  305.8 48.7 %copy-start = (bf16[96,12288]{1,0:T(8,128)(2,1)S(1)}, bf16[96,12288]{1,0:T(8,128)(2,1)}, u32[]{:S(2)}) copy-start(bf16[96,12288]{1,0:T(8,128)(2,1)} %get-tuple-element.17) | copy-start | bytes 7077892
